TPU v7x, 32 devices: a whole 2x2x4 slice. The times are simulated.
32 devices in a mesh: section: 4 (over y, x), seq: 8 (over z, core).
Axes of the slice: x: 2, y: 2, z: 4, core: 2. Of those that a mesh axis runs over, the one named last changes fastest.
Arguments:
- stream: bfloat16 [4, 1024, 4096], P('section', 'seq'), may hold values from -4 to 4
- queries: bfloat16 [4, 1024, 4096], P('section', 'seq')
- span_kv: bfloat16 [4, 2, 1024, 512], P('section', None, 'seq')
- cache_kv: bfloat16 [4, 2, 1024, 512], P('section', None, 'seq'), may hold values from -6 to 6
- cache_len: int32 [8], replicated, may hold values from 48 to 80, as said below
- context_start: int32 [1], replicated, may hold values from 1 to 1024
- block_table: int32 [8, 8], replicated, may hold values from 0 to 1, as said below
Outputs:
- handed: bfloat16 [4, 1024, 4096], P('section', 'seq')
Inputs may be any that keep to these rules, and one draw needn't show every extreme that they name: `cache_len`: some index holds exactly 80 live slots. `block_table`: the diagonal is 1 and every entry above it is 0.
All inputs are finite; a program needn't handle non-finite values.
Results may differ from a plain program's by a relative error of at most 0.006.
Values may be sent and summed in bfloat16 or wider, within the bound.
A program may use at most 64 MiB of HBM per device.

v0:
```python
import functools
import math

import jax
import jax.numpy as jnp
from jax import lax
from jax.experimental import pallas as pl
from jax.experimental.pallas import tpu as pltpu
from jax.sharding import PartitionSpec as P

HEAD_DIM = 128
LIVE_MAX = 80
TILE_HEADS = 2
BLOCK_HEADS = 8
CACHE, SPAN = 0, 1
UP, DOWN, SIDE = 0, 1, 2
MESH = pl.DeviceIdType.MESH


def kernel(
    seq_count, section_count, kv_count, group_size, tok_rows, slot_rows,
    len_ref, start_ref, table_ref, stream_hbm, query_hbm, span_hbm, cache_hbm,
    out_hbm,
    cache_all, span_all, query_v, stream_v, stage, cache_scores, span_scores,
    cache_bias, span_bias, top_v, acc_v,
    local_sem, bulk_sem, send_sem, recv_sem, hand_send, hand_recv,
):
    section = lax.axis_index("section")
    me = lax.axis_index("seq")
    chip_count = seq_count // 2
    chip = me // 2
    parity = me - chip * 2
    partner = me + 1 - 2 * parity
    has_up = chip < chip_count - 1
    has_down = chip > 0
    next_section = lax.rem(section + 1, section_count)
    prev_section = lax.rem(section + section_count - 1, section_count)
    tile_cols = TILE_HEADS * HEAD_DIM
    tiles_per = BLOCK_HEADS // TILE_HEADS
    blocks_per = group_size // BLOCK_HEADS
    pair_keys = 2 * tok_rows
    cache_rows = seq_count * LIVE_MAX
    cache_chunk = math.gcd(seq_count, 8) * LIVE_MAX
    cache_chunks = cache_rows // cache_chunk

    def piece(kind, head, shard):
        if kind == CACHE:
            rows = pl.ds(pl.multiple_of(shard * LIVE_MAX, 16), LIVE_MAX)
            return cache_all.at[head, :, rows, :]
        rows = pl.ds(pl.multiple_of(shard * tok_rows, 16), tok_rows)
        return span_all.at[head, :, rows, :]

    def local_copy(kind, head):
        cols = pl.ds(pl.multiple_of(head * HEAD_DIM, HEAD_DIM), HEAD_DIM)
        if kind == CACHE:
            source = cache_hbm.at[0, :, pl.ds(0, LIVE_MAX), cols]
        else:
            source = span_hbm.at[0, :, :, cols]
        return pltpu.make_async_copy(source, piece(kind, head, me), local_sem.at[kind, head])

    def link(way, kind, head, shard):
        target = {UP: me + 2, DOWN: me - 2, SIDE: partner}[way]
        ref = piece(kind, head, shard)
        return pltpu.make_async_remote_copy(
            src_ref=ref, dst_ref=ref,
            send_sem=send_sem.at[way, kind, head, shard],
            recv_sem=recv_sem.at[kind, head, shard],
            device_id={"seq": target}, device_id_type=MESH,
        )

    def hand(tile):
        cols = pl.ds(pl.multiple_of(tile * tile_cols, tile_cols), tile_cols)
        return pltpu.make_async_remote_copy(
            src_ref=stage.at[:, cols], dst_ref=out_hbm.at[0, :, cols],
            send_sem=hand_send.at[tile], recv_sem=hand_recv.at[tile],
            device_id={"section": next_section}, device_id_type=MESH,
        )

    for head in range(kv_count):
        local_copy(CACHE, head).start()
        local_copy(SPAN, head).start()
    query_copy = pltpu.make_async_copy(query_hbm.at[0], query_v, bulk_sem.at[0])
    stream_copy = pltpu.make_async_copy(stream_hbm.at[0], stream_v, bulk_sem.at[1])
    query_copy.start()
    stream_copy.start()

    barrier = pltpu.get_barrier_semaphore()

    def greet(device):
        pl.semaphore_signal(barrier, inc=1, device_id=device, device_id_type=MESH)

    greet({"seq": partner})
    greet({"section": next_section})
    greet({"section": prev_section})

    @pl.when(has_up)
    def _():
        greet({"seq": me + 2})

    @pl.when(has_down)
    def _():
        greet({"seq": me - 2})

    key_col = lax.broadcasted_iota(jnp.int32, (1, cache_rows), 1)
    owner = jnp.zeros((1, cache_rows), jnp.int32)
    live = jnp.full((1, cache_rows), len_ref[0], jnp.int32)
    for shard in range(1, seq_count):
        later = key_col >= shard * LIVE_MAX
        owner = jnp.where(later, shard, owner)
        live = jnp.where(later, len_ref[shard], live)
    slot = key_col - owner * LIVE_MAX
    first_visible = slot_rows * seq_count - start_ref[0]
    cache_open = (slot < live) & (owner * slot_rows + slot >= first_visible)
    cache_bias[...] = jnp.where(cache_open, 0.0, -jnp.inf).astype(jnp.float32)
    pair_col = lax.broadcasted_iota(jnp.int32, (1, pair_keys), 1)
    for pair in range(chip_count):
        hits = jnp.where(pair_col < tok_rows, table_ref[me, 2 * pair], table_ref[me, 2 * pair + 1])
        span_bias[pair, :, :] = jnp.where(hits == 1, 0.0, -jnp.inf).astype(jnp.float32)

    pl.semaphore_wait(barrier, 3 + has_up.astype(jnp.int32) + has_down.astype(jnp.int32))

    def send_own(head):
        local_copy(CACHE, head).wait()
        local_copy(SPAN, head).wait()

        @pl.when(has_up)
        def _():
            link(UP, CACHE, head, me).start()
            link(UP, SPAN, head, me).start()

        @pl.when(has_down)
        def _():
            link(DOWN, CACHE, head, me).start()

        link(SIDE, CACHE, head, me).start()
        link(SIDE, SPAN, head, me).start()

    def relay(head):
        @pl.loop(1, chip_count)
        def _(step):
            @pl.when(step <= chip)
            def _():
                shard = me - 2 * step
                for kind in (CACHE, SPAN):
                    link(UP, kind, head, shard).wait_recv()

                    @pl.when(has_up)
                    def _():
                        link(UP, kind, head, shard).start()

                    link(SIDE, kind, head, shard).start()

            @pl.when(chip + step < chip_count)
            def _():
                shard = me + 2 * step
                link(DOWN, CACHE, head, shard).wait_recv()

                @pl.when(has_down)
                def _():
                    link(DOWN, CACHE, head, shard).start()

                link(SIDE, CACHE, head, shard).start()

    def from_partner(head):
        @pl.loop(0, chip_count)
        def _(other):
            shard = partner + 2 * (other - chip)
            link(SIDE, CACHE, head, shard).wait_recv()

            @pl.when(other <= chip)
            def _():
                link(SIDE, SPAN, head, shard).wait_recv()

    factor = math.log2(math.e) / math.sqrt(HEAD_DIM)

    def query_key(rows, keys):
        return lax.dot_general(
            rows, keys, (((1,), (1,)), ((), ())), preferred_element_type=jnp.float32
        )

    def lane_top(scores):
        best = scores[:, :HEAD_DIM]
        for first in range(HEAD_DIM, scores.shape[1], HEAD_DIM):
            best = jnp.maximum(best, scores[:, first : first + HEAD_DIM])
        return best

    def weighted(scores, values):
        tops = jnp.concatenate([top_v[...]] * (scores.shape[1] // HEAD_DIM), axis=1)
        weights = jnp.exp2((scores - tops) * factor).astype(jnp.bfloat16)
        wide = jnp.concatenate([values, jnp.ones_like(values)], axis=1)
        return jnp.dot(weights, wide, preferred_element_type=jnp.float32)

    def cache_part(chunk):
        return pl.ds(pl.multiple_of(chunk * cache_chunk, 16), cache_chunk)

    def cache_lanes(chunk):
        if cache_chunks == 1:
            return pl.ds(0, cache_chunk)
        return pl.ds(pl.multiple_of(chunk * cache_chunk, HEAD_DIM), cache_chunk)

    def span_part(pair):
        return pl.ds(pl.multiple_of(pair * pair_keys, HEAD_DIM), pair_keys)

    def attend(head, block):
        def cols(index):
            first = (block * BLOCK_HEADS + index) * HEAD_DIM
            return pl.ds(pl.multiple_of(first, HEAD_DIM), HEAD_DIM)

        def rows():
            return jnp.concatenate([query_v[:, cols(i)] for i in range(BLOCK_HEADS)], axis=0)

        scores = query_key(rows(), span_all[head, 0, span_part(chip), :]) + span_bias[chip]
        token = lax.broadcasted_iota(jnp.int32, (tok_rows, pair_keys), 0) + parity * tok_rows
        key = lax.broadcasted_iota(jnp.int32, (tok_rows, pair_keys), 1)
        causal = jnp.concatenate([key <= token] * BLOCK_HEADS, axis=0)
        scores = jnp.where(causal, scores, -jnp.inf)
        span_scores[:, span_part(chip)] = scores
        top_v[...] = lane_top(scores)

        def span_scored(pair, _):
            scores = query_key(rows(), span_all[head, 0, span_part(pair), :]) + span_bias[pair]
            span_scores[:, span_part(pair)] = scores
            top_v[...] = jnp.maximum(top_v[...], lane_top(scores))
            return 0

        def cache_scored(chunk, _):
            scores = query_key(rows(), cache_all[head, 0, cache_part(chunk), :])
            scores = scores + cache_bias[:, cache_lanes(chunk)]
            cache_scores[:, cache_lanes(chunk)] = scores
            top_v[...] = jnp.maximum(top_v[...], lane_top(scores))
            return 0

        lax.fori_loop(0, cache_chunks, cache_scored, 0)
        lax.fori_loop(0, chip, span_scored, 0)
        row_top = jnp.max(top_v[...], axis=1, keepdims=True)
        top_v[...] = jnp.broadcast_to(row_top, top_v.shape)

        def cache_mixed(chunk):
            return weighted(cache_scores[:, cache_lanes(chunk)], cache_all[head, 1, cache_part(chunk), :])

        def span_mixed(pair):
            return weighted(span_scores[:, span_part(pair)], span_all[head, 1, span_part(pair), :])

        def cache_added(chunk, _):
            acc_v[...] += cache_mixed(chunk)
            return 0

        def span_added(pair, _):
            acc_v[...] += span_mixed(pair)
            return 0

        acc_v[...] = cache_mixed(0)
        if cache_chunks > 1:
            lax.fori_loop(1, cache_chunks, cache_added, 0)
        lax.fori_loop(0, chip + 1, span_added, 0)

    def finish(tile, part):
        for index in range(TILE_HEADS):
            first = pl.multiple_of((part * TILE_HEADS + index) * tok_rows, tok_rows)
            mixed = acc_v[pl.ds(first, tok_rows), :]
            attn = (mixed[:, :HEAD_DIM] / mixed[:, HEAD_DIM:]).astype(jnp.bfloat16)
            first = (tile * TILE_HEADS + index) * HEAD_DIM
            cols = pl.ds(pl.multiple_of(first, HEAD_DIM), HEAD_DIM)
            total = stream_v[:, cols].astype(jnp.float32) + attn.astype(jnp.float32)
            stage[:, cols] = total.astype(jnp.bfloat16)

    send_own(0)
    send_own(1)
    query_copy.wait()
    stream_copy.wait()

    @pl.loop(0, kv_count)
    def _(head):
        relay(head)

        @pl.when(head + 2 < kv_count)
        def _():
            send_own(head + 2)

        from_partner(head)

        @pl.loop(0, blocks_per)
        def _(inner):
            block = head * blocks_per + inner
            attend(head, block)

            @pl.loop(0, tiles_per)
            def _(part):
                tile = block * tiles_per + part
                finish(tile, part)

                @pl.when(tile > 0)
                def _():
                    hand(tile - 1).start()

    @pl.loop(0, kv_count)
    def _(head):
        @pl.loop(0, chip_count)
        def _(other):
            shard = parity + 2 * other
            link(SIDE, CACHE, head, shard).wait_send()

            @pl.when(other <= chip)
            def _():
                link(SIDE, SPAN, head, shard).wait_send()

                @pl.when(has_up)
                def _():
                    link(UP, CACHE, head, shard).wait_send()
                    link(UP, SPAN, head, shard).wait_send()

            @pl.when((other >= chip) & has_down)
            def _():
                link(DOWN, CACHE, head, shard).wait_send()

    tile_count = kv_count * group_size // TILE_HEADS
    hand(tile_count - 1).start()

    @pl.loop(0, tile_count)
    def _(tile):
        hand(tile).wait_recv()
        hand(tile).wait_send()


def shards(stream, queries, span_kv, cache_kv, cache_len, context_start, block_table):
    seq_count = lax.axis_size("seq")
    section_count = lax.axis_size("section")
    tok_rows, query_width = queries.shape[1:]
    key_width = span_kv.shape[3]
    kv_count = key_width // HEAD_DIM
    group_size = query_width // key_width
    slot_rows = cache_kv.shape[2]
    block_rows = BLOCK_HEADS * tok_rows
    tile_count = kv_count * group_size // TILE_HEADS
    smem = pl.BlockSpec(memory_space=pltpu.SMEM)
    hbm = pl.BlockSpec(memory_space=pl.ANY)
    bf16, f32 = jnp.bfloat16, jnp.float32
    return pl.pallas_call(
        functools.partial(
            kernel, seq_count, section_count, kv_count, group_size, tok_rows, slot_rows
        ),
        out_shape=jax.ShapeDtypeStruct(stream.shape, bf16),
        in_specs=[smem] * 3 + [hbm] * 4,
        out_specs=hbm,
        scratch_shapes=[
            pltpu.VMEM((kv_count, 2, seq_count * LIVE_MAX, HEAD_DIM), bf16),
            pltpu.VMEM((kv_count, 2, seq_count * tok_rows, HEAD_DIM), bf16),
            pltpu.VMEM((tok_rows, query_width), bf16),
            pltpu.VMEM((tok_rows, query_width), bf16),
            pltpu.VMEM((tok_rows, query_width), bf16),
            pltpu.VMEM((block_rows, seq_count * LIVE_MAX), f32),
            pltpu.VMEM((block_rows, seq_count * tok_rows), f32),
            pltpu.VMEM((1, seq_count * LIVE_MAX), f32),
            pltpu.VMEM((seq_count // 2, 1, 2 * tok_rows), f32),
            pltpu.VMEM((block_rows, HEAD_DIM), f32),
            pltpu.VMEM((block_rows, 2 * HEAD_DIM), f32),
            pltpu.SemaphoreType.DMA((2, kv_count)),
            pltpu.SemaphoreType.DMA((2,)),
            pltpu.SemaphoreType.DMA((3, 2, kv_count, seq_count)),
            pltpu.SemaphoreType.DMA((2, kv_count, seq_count)),
            pltpu.SemaphoreType.DMA((tile_count,)),
            pltpu.SemaphoreType.DMA((tile_count,)),
        ],
        compiler_params=pltpu.CompilerParams(collective_id=0, has_side_effects=True),
    )(cache_len, context_start, block_table, stream, queries, span_kv, cache_kv)


def solution(mesh):
    return jax.shard_map(
        shards,
        mesh=mesh,
        in_specs=(
            P("section", "seq", None),
            P("section", "seq", None),
            P("section", None, "seq", None),
            P("section", None, "seq", None),
            P(),
            P(),
            P(),
        ),
        out_specs=P("section", "seq", None),
        check_vma=False,
    )
```

profile of v0, /device:TPU:0, one launch (start us, length us, event | category | flops | bytes accessed | tf_op | source)
XLA Modules:
  0.0 56.5 jit_solution(18418864696647106663)
XLA Ops:
  0.7 53.5 %shard_map.73 = bf16[1,128,4096]{2,1,0:T(8,128)(2,1)} custom-call(s32[8]{0:T(128)} %len_ref.1, s32[1]{0:T(128)S(6)} %copy.9.start_ref, s32[8,8]{1,0:T(8,128)} %table_ref.1, bf16[1,128,4096]{2,1,0:T(8,128)(2,1)} %stream_hbm.1, bf16[1,128,4096]{2,1,0:T(8,128)(2,1)} %query_hbm.1, bf16[1,2,128,512]{3,2,1,0:T(8,128)(2,1)} %span_hbm.1, ...), custom_call_target="tpu_custom_call" | custom-call | tf_op jit(solution)/shard_map/pallas_call | solution.py:338
  54.2 2.3 %copy.10 = bf16[1,128,4096]{2,1,0:T(8,128)(2,1)} copy(bf16[1,128,4096]{2,1,0:T(8,128)(2,1)} %shard_map.73) | data formatting | bytes 2097152
where the time goes:
time: 56.7 us; the launch traced here: 56.5 us
  Pallas kernels  53.5 us (94%)
  local copies, waits for them, and re-layouts  2.29 us (4%)
  between operations  0.66 us (1%)
    pallas_call x1, Pallas kernels, shards(): pl.pallas_call(functools.partial(kernel, seq_count, section_count, kv_cou...  53.5 us
    unnamed x1, local copies, waits for them, and re-layouts  2.29 us

commit v1 on v0

v1 whole, which is shorter than its diff:
```python
import functools
import math

import jax
import jax.numpy as jnp
from jax import lax
from jax.experimental import pallas as pl
from jax.experimental.pallas import tpu as pltpu
from jax.sharding import PartitionSpec as P

HEAD_DIM = 128
LIVE_MAX = 80
TILE_HEADS = 2
BLOCK_HEADS = 4
LEVELS = 1
CHUNK_SHARDS = 8
FULL, CACHE, SPAN = 0, 1, 2
MESH = pl.DeviceIdType.MESH


def round_up(value, step):
    return -(-value // step) * step


def kernel(
    sizes, first_chip,
    len_ref, start_ref, table_ref, stream_hbm, query_hbm, span_hbm, cache_hbm,
    out_ref,
    pairs_all, query_v, stream_v, stage, cache_scores, span_scores,
    cache_bias, span_bias, top_v, acc_v,
    local_sem, bulk_sem, up_sem, side_sem, down_sem, recv_sem, hand_send, hand_recv,
):
    seq_count, section_count, kv_count, group_size, tok_rows, slot_rows = sizes
    section = lax.axis_index("section")
    me = lax.axis_index("seq")
    chip_count = seq_count // 2
    chip = me // 2
    parity = me - chip * 2
    partner = me + 1 - 2 * parity
    has_up = chip < chip_count - 1
    next_section = lax.rem(section + 1, section_count)
    prev_section = lax.rem(section + section_count - 1, section_count)
    tile_cols = TILE_HEADS * HEAD_DIM
    tiles_per = BLOCK_HEADS // TILE_HEADS
    blocks_per = group_size // BLOCK_HEADS
    pair_keys = 2 * tok_rows
    span_start = 2 * LIVE_MAX
    shard_rows = span_start + 2 * tok_rows
    first_shard = 2 * first_chip
    open_shards = seq_count - first_shard
    chunk_shards = open_shards if open_shards <= CHUNK_SHARDS else math.gcd(open_shards, CHUNK_SHARDS)
    chunk_keys = chunk_shards * LIVE_MAX
    chunk_lanes = round_up(chunk_keys, HEAD_DIM)
    chunks = open_shards // chunk_shards if open_shards else 0

    def piece(kind, head, shard):
        first, count = {
            FULL: (0, shard_rows), CACHE: (0, span_start), SPAN: (span_start, 2 * tok_rows)
        }[kind]
        return pairs_all.at[head, shard, pl.ds(first, count), :]

    def lower(source_chip, act):
        if first_chip == 0:
            act(FULL)
        elif first_chip == chip_count:
            act(SPAN)
        else:

            @pl.when(source_chip >= first_chip)
            def _():
                act(FULL)

            @pl.when(source_chip < first_chip)
            def _():
                act(SPAN)

    def upper(source_chip, act):
        if first_chip == 0:
            act(CACHE)
        elif first_chip < chip_count:

            @pl.when(source_chip >= first_chip)
            def _():
                act(CACHE)

    def local_copies(head):
        cols = pl.ds(pl.multiple_of(head * HEAD_DIM, HEAD_DIM), HEAD_DIM)
        parts = []
        for which in range(2):
            rows = pl.ds(which * LIVE_MAX, LIVE_MAX)
            parts.append((cache_hbm.at[0, which, pl.ds(0, LIVE_MAX), cols], rows))
            rows = pl.ds(span_start + which * tok_rows, tok_rows)
            parts.append((span_hbm.at[0, which, :, cols], rows))
        return [
            pltpu.make_async_copy(source, pairs_all.at[head, me, rows, :], local_sem.at[i, head])
            for i, (source, rows) in enumerate(parts)
        ]

    def remote(kind, head, shard, send, target):
        ref = piece(kind, head, shard)
        return pltpu.make_async_remote_copy(
            src_ref=ref, dst_ref=ref, send_sem=send, recv_sem=recv_sem.at[head, shard],
            device_id={"seq": target}, device_id_type=MESH,
        )

    def go_up(kind, head, shard):
        return remote(kind, head, shard, up_sem.at[head, shard], me + 2)

    def go_side(kind, head, shard):
        return remote(kind, head, shard, side_sem.at[head, shard], partner)

    def go_down(head, other):
        return remote(CACHE, head, me, down_sem.at[head, other], parity + 2 * other)

    def hand(tile):
        cols = pl.ds(pl.multiple_of(tile * tile_cols, tile_cols), tile_cols)
        return pltpu.make_async_remote_copy(
            src_ref=stage.at[:, cols], dst_ref=out_ref.at[0, :, cols],
            send_sem=hand_send.at[tile], recv_sem=hand_recv.at[tile],
            device_id={"section": next_section}, device_id_type=MESH,
        )

    for head in range(kv_count):
        for copy in local_copies(head):
            copy.start()
    query_copy = pltpu.make_async_copy(query_hbm.at[0], query_v, bulk_sem.at[0])
    stream_copy = pltpu.make_async_copy(stream_hbm.at[0], stream_v, bulk_sem.at[1])
    query_copy.start()
    stream_copy.start()

    barrier = pltpu.get_barrier_semaphore()

    def greet(device):
        pl.semaphore_signal(barrier, inc=1, device_id=device, device_id_type=MESH)

    @pl.loop(0, chip_count)
    def _(other):
        @pl.when(other != chip)
        def _():
            greet({"seq": parity + 2 * other})

    greet({"seq": partner})
    greet({"section": next_section})
    greet({"section": prev_section})

    first_visible = slot_rows * seq_count - start_ref[0]
    for chunk in range(chunks):
        key_col = lax.broadcasted_iota(jnp.int32, (1, chunk_lanes), 1)
        begin = first_shard + chunk * chunk_shards
        owner = jnp.full((1, chunk_lanes), begin, jnp.int32)
        live = jnp.full((1, chunk_lanes), len_ref[begin], jnp.int32)
        for step in range(1, chunk_shards):
            later = key_col >= step * LIVE_MAX
            owner = jnp.where(later, begin + step, owner)
            live = jnp.where(later, len_ref[begin + step], live)
        slot = key_col - (owner - begin) * LIVE_MAX
        cache_open = (slot < live) & (slot < LIVE_MAX)
        cache_open = cache_open & (owner * slot_rows + slot >= first_visible)
        lanes = pl.ds(chunk * chunk_lanes, chunk_lanes)
        cache_bias[:, lanes] = jnp.where(cache_open, 0.0, -jnp.inf).astype(jnp.float32)
    pair_col = lax.broadcasted_iota(jnp.int32, (1, pair_keys), 1)
    for pair in range(chip_count):
        hits = jnp.where(pair_col < tok_rows, table_ref[me, 2 * pair], table_ref[me, 2 * pair + 1])
        span_bias[pair, :, :] = jnp.where(hits == 1, 0.0, -jnp.inf).astype(jnp.float32)

    pl.semaphore_wait(barrier, chip_count - 1 + 3)

    def send_up(head):
        @pl.when(has_up)
        def _():
            lower(chip, lambda kind: go_up(kind, head, me).start())

    def send_rest(head):
        lower(chip, lambda kind: go_side(kind, head, me).start())

        @pl.loop(1, chip_count)
        def _(step):
            @pl.when(step <= chip)
            def _():
                upper(chip, lambda kind: go_down(head, chip - step).start())

    def relay(head):
        @pl.loop(1, chip_count)
        def _(step):
            @pl.when(step <= chip)
            def _():
                shard = me - 2 * step

                def act(kind):
                    go_up(kind, head, shard).wait_recv()

                    @pl.when(has_up)
                    def _():
                        go_up(kind, head, shard).start()

                    go_side(kind, head, shard).start()

                lower(chip - step, act)

    def from_above(head):
        @pl.loop(1, chip_count)
        def _(step):
            @pl.when(chip + step < chip_count)
            def _():
                shard = me + 2 * step

                def act(kind):
                    go_side(kind, head, shard).wait_recv()
                    go_side(kind, head, shard).start()

                upper(chip + step, act)

    def from_partner(head):
        @pl.loop(0, chip_count)
        def _(other):
            shard = partner + 2 * (other - chip)

            def act(kind):
                go_side(kind, head, shard).wait_recv()

            @pl.when(other <= chip)
            def _():
                lower(other, act)

            @pl.when(other > chip)
            def _():
                upper(other, act)

    factor = math.log2(math.e) / math.sqrt(HEAD_DIM)

    def query_key(rows, keys):
        return lax.dot_general(
            rows, keys, (((1,), (1,)), ((), ())), preferred_element_type=jnp.float32
        )

    def lane_top(scores):
        best = scores[:, :HEAD_DIM]
        for first in range(HEAD_DIM, scores.shape[1], HEAD_DIM):
            best = jnp.maximum(best, scores[:, first : first + HEAD_DIM])
        return best

    def weighted(scores, values):
        tops = jnp.concatenate([top_v[...]] * (scores.shape[1] // HEAD_DIM), axis=1)
        weights = jnp.exp2((scores - tops) * factor).astype(jnp.bfloat16)
        wide = jnp.concatenate([values, jnp.ones_like(values)], axis=1)
        return jnp.dot(weights, wide, preferred_element_type=jnp.float32)

    def cache_part(head, chunk, which):
        begin = first_shard + chunk * chunk_shards
        part = pairs_all[head, pl.ds(begin, chunk_shards), pl.ds(which * LIVE_MAX, LIVE_MAX), :]
        part = part.reshape(chunk_keys, HEAD_DIM)
        if chunk_lanes > chunk_keys:
            blank = jnp.zeros((chunk_lanes - chunk_keys, HEAD_DIM), part.dtype)
            part = jnp.concatenate([part, blank], axis=0)
        return part

    def cache_lanes(chunk):
        if chunks == 1:
            return pl.ds(0, chunk_lanes)
        return pl.ds(pl.multiple_of(chunk * chunk_lanes, HEAD_DIM), chunk_lanes)

    def span_part(head, pair, which):
        rows = pl.ds(span_start + which * tok_rows, tok_rows)
        return pairs_all[head, pl.ds(2 * pair, 2), rows, :].reshape(pair_keys, HEAD_DIM)

    def span_lanes(pair):
        return pl.ds(pl.multiple_of(pair * pair_keys, HEAD_DIM), pair_keys)

    def attend(head, block):
        def cols(index):
            first = (block * BLOCK_HEADS + index) * HEAD_DIM
            return pl.ds(pl.multiple_of(first, HEAD_DIM), HEAD_DIM)

        def rows():
            return jnp.concatenate([query_v[:, cols(i)] for i in range(BLOCK_HEADS)], axis=0)

        scores = query_key(rows(), span_part(head, chip, 0)) + span_bias[chip]
        token = lax.broadcasted_iota(jnp.int32, (tok_rows, pair_keys), 0) + parity * tok_rows
        key = lax.broadcasted_iota(jnp.int32, (tok_rows, pair_keys), 1)
        causal = jnp.concatenate([key <= token] * BLOCK_HEADS, axis=0)
        scores = jnp.where(causal, scores, -jnp.inf)
        span_scores[:, span_lanes(chip)] = scores
        top_v[...] = lane_top(scores)

        def span_scored(pair, _):
            scores = query_key(rows(), span_part(head, pair, 0)) + span_bias[pair]
            span_scores[:, span_lanes(pair)] = scores
            top_v[...] = jnp.maximum(top_v[...], lane_top(scores))
            return 0

        def cache_scored(chunk, _):
            scores = query_key(rows(), cache_part(head, chunk, 0))
            scores = scores + cache_bias[:, cache_lanes(chunk)]
            cache_scores[:, cache_lanes(chunk)] = scores
            top_v[...] = jnp.maximum(top_v[...], lane_top(scores))
            return 0

        if chunks:
            lax.fori_loop(0, chunks, cache_scored, 0)
        lax.fori_loop(0, chip, span_scored, 0)
        row_top = jnp.max(top_v[...], axis=1, keepdims=True)
        top_v[...] = jnp.broadcast_to(row_top, top_v.shape)

        def cache_mixed(chunk):
            return weighted(cache_scores[:, cache_lanes(chunk)], cache_part(head, chunk, 1))

        def span_mixed(pair):
            return weighted(span_scores[:, span_lanes(pair)], span_part(head, pair, 1))

        def cache_added(chunk, _):
            acc_v[...] += cache_mixed(chunk)
            return 0

        def span_added(pair, _):
            acc_v[...] += span_mixed(pair)
            return 0

        acc_v[...] = span_mixed(chip)
        if chunks:
            lax.fori_loop(0, chunks, cache_added, 0)
        lax.fori_loop(0, chip, span_added, 0)

    def finish(tile, part):
        for index in range(TILE_HEADS):
            first = pl.multiple_of((part * TILE_HEADS + index) * tok_rows, tok_rows)
            mixed = acc_v[pl.ds(first, tok_rows), :]
            attn = (mixed[:, :HEAD_DIM] / mixed[:, HEAD_DIM:]).astype(jnp.bfloat16)
            first = (tile * TILE_HEADS + index) * HEAD_DIM
            cols = pl.ds(pl.multiple_of(first, HEAD_DIM), HEAD_DIM)
            total = stream_v[:, cols].astype(jnp.float32) + attn.astype(jnp.float32)
            stage[:, cols] = total.astype(jnp.bfloat16)

    for head in range(kv_count):
        for copy in local_copies(head):
            copy.wait()
        if head < 2:
            send_up(head)
        send_rest(head)
    query_copy.wait()
    stream_copy.wait()

    @pl.loop(0, kv_count)
    def _(head):
        relay(head)

        @pl.when(head + 2 < kv_count)
        def _():
            send_up(head + 2)

        from_above(head)
        from_partner(head)

        @pl.loop(0, blocks_per)
        def _(inner):
            block = head * blocks_per + inner
            attend(head, block)

            @pl.loop(0, tiles_per)
            def _(part):
                tile = block * tiles_per + part
                finish(tile, part)

                @pl.when(tile > 0)
                def _():
                    hand(tile - 1).start()

    @pl.loop(0, kv_count)
    def _(head):
        @pl.loop(0, chip_count)
        def _(other):
            shard = parity + 2 * other

            @pl.when(other <= chip)
            def _():
                def act(kind):
                    go_side(kind, head, shard).wait_send()

                    @pl.when(has_up)
                    def _():
                        go_up(kind, head, shard).wait_send()

                lower(other, act)

            @pl.when(other < chip)
            def _():
                upper(chip, lambda kind: go_down(head, other).wait_send())

            @pl.when(other > chip)
            def _():
                upper(other, lambda kind: go_side(kind, head, shard).wait_send())

    tile_count = kv_count * group_size // TILE_HEADS
    hand(tile_count - 1).start()

    @pl.loop(0, tile_count)
    def _(tile):
        hand(tile).wait_recv()
        hand(tile).wait_send()


def shards(stream, queries, span_kv, cache_kv, cache_len, context_start, block_table):
    seq_count = lax.axis_size("seq")
    section_count = lax.axis_size("section")
    tok_rows, query_width = queries.shape[1:]
    key_width = span_kv.shape[3]
    kv_count = key_width // HEAD_DIM
    group_size = query_width // key_width
    slot_rows = cache_kv.shape[2]
    block_rows = BLOCK_HEADS * tok_rows
    tile_count = kv_count * group_size // TILE_HEADS
    chip_count = seq_count // 2
    sizes = (seq_count, section_count, kv_count, group_size, tok_rows, slot_rows)
    smem = pl.BlockSpec(memory_space=pltpu.SMEM)
    hbm = pl.BlockSpec(memory_space=pl.ANY)
    vmem = pl.BlockSpec(memory_space=pltpu.VMEM)
    bf16, f32 = jnp.bfloat16, jnp.float32
    dma = pltpu.SemaphoreType.DMA
    cache_width = seq_count * round_up(LIVE_MAX, HEAD_DIM)

    def call(level):
        return pl.pallas_call(
            functools.partial(kernel, sizes, level * chip_count // LEVELS),
            out_shape=pltpu.VMEM(stream.shape, bf16),
            in_specs=[smem] * 3 + [hbm] * 4,
            out_specs=vmem,
            scratch_shapes=[
                pltpu.VMEM((kv_count, seq_count, 2 * (LIVE_MAX + tok_rows), HEAD_DIM), bf16),
                pltpu.VMEM((tok_rows, query_width), bf16),
                pltpu.VMEM((tok_rows, query_width), bf16),
                pltpu.VMEM((tok_rows, query_width), bf16),
                pltpu.VMEM((block_rows, cache_width), f32),
                pltpu.VMEM((block_rows, seq_count * tok_rows), f32),
                pltpu.VMEM((1, cache_width), f32),
                pltpu.VMEM((chip_count, 1, 2 * tok_rows), f32),
                pltpu.VMEM((block_rows, HEAD_DIM), f32),
                pltpu.VMEM((block_rows, 2 * HEAD_DIM), f32),
                dma((4, kv_count)),
                dma((2,)),
                dma((kv_count, seq_count)),
                dma((kv_count, seq_count)),
                dma((kv_count, chip_count)),
                dma((kv_count, seq_count)),
                dma((tile_count,)),
                dma((tile_count,)),
            ],
            compiler_params=pltpu.CompilerParams(collective_id=level, has_side_effects=True),
        )(cache_len, context_start, block_table, stream, queries, span_kv, cache_kv)

    return call(0)


def solution(mesh):
    return jax.shard_map(
        shards,
        mesh=mesh,
        in_specs=(
            P("section", "seq", None),
            P("section", "seq", None),
            P("section", None, "seq", None),
            P("section", None, "seq", None),
            P(),
            P(),
            P(),
        ),
        out_specs=P("section", "seq", None),
        check_vma=False,
    )
```

time: 56.7 us -> 53.8 us (0.949)
  the two profiles are of different devices: /device:TPU:0 before, /device:TPU:25 now
where the time goes in v1:
time: 53.8 us; the launch traced here: 53.6 us
  Pallas kernels  52 us (97%)
  local copies, waits for them, and re-layouts  0.97 us (2%)
  between operations  0.66 us (1%)
    pallas_call x1, Pallas kernels, call(): pl.pallas_call(functools.partial(kernel, sizes, level * chip_count // LEV...  52 us

profile of v1, /device:TPU:25, one launch (start us, length us, event | category | flops | bytes accessed | tf_op | source)
XLA Modules:
  0.0 53.6 jit_solution(5155377058660861694)
XLA Ops:
  0.7 52.0 %shard_map.73 = bf16[1,128,4096]{2,1,0:T(8,128)(2,1)S(1)} custom-call(s32[8]{0:T(128)} %len_ref.1, s32[1]{0:T(128)S(6)} %copy.10.start_ref, s32[8,8]{1,0:T(8,128)} %table_ref.1, bf16[1,128,4096]{2,1,0:T(8,128)(2,1)} %stream_hbm.1, bf16[1,128,4096]{2,1,0:T(8,128)(2,1)} %query_hbm.1, bf16[1,2,128,512]{3,2,1,0:T(8,128)(2,1)} %span_hbm.1, ...), custom_call_target="tpu_custom_call" | custom-call | tf_op jit(solution)/shard_map/pallas_call | solution.py:421
  52.6 1.0 %copy.9 = bf16[1,128,4096]{2,1,0:T(8,128)(2,1)} copy(bf16[1,128,4096]{2,1,0:T(8,128)(2,1)S(1)} %shard_map.73) | data formatting | bytes 2097152
